TPU v7x, 256 devices: a whole 4x4x8 slice. The times are simulated.
256 devices in a mesh: pop: 16 (over y, z_hi, core), col: 16 (over z_lo, x).
Axes of the slice: x: 4, y: 4, z: 8 (z_hi: 2, z_lo: 4; z = z_hi * 4 + z_lo), core: 2. Of those that a mesh axis runs over, the one named last changes fastest.
Arguments:
- tokens: bfloat16 [14336, 4096], P('pop'), may hold values from -6 to 6
- weight: bfloat16 [4096, 16384], P(None, ('col', 'pop')), may hold values from -0.09375 to 0.09375
- old_left: bfloat16 [1792, 4, 4096], P('pop', None, 'col'), may hold values from -6 to 6
- old_right: bfloat16 [1792, 4, 16384], P('pop', None, 'col'), may hold values from -6 to 6
- selected: int32 [16, 8], P('pop'), may hold values from 0 to 111, as said below
- shaping: float32 [16, 8], P('pop'), may hold values from -3 to 3
- new_left: bfloat16 [1792, 4, 4096], P('pop', None, 'col'), may hold values from -6 to 6
- new_right: bfloat16 [1792, 4, 16384], P('pop', None, 'col'), may hold values from -6 to 6
Outputs:
- updated: bfloat16 [4096, 16384], P(None, ('col', 'pop'))
- activations: bfloat16 [14336, 16384], P('pop', 'col')
Inputs may be any that keep to these rules, and one draw needn't show every extreme that they name: `selected`: each row names 8 different members of its group.
All inputs are finite; a program needn't handle non-finite values.
Results may differ from a plain program's by a relative error of at most 0.0055.
Values may be sent and summed in bfloat16 or wider, within the bound.
A program may use at most 128 MiB of HBM per device.

v0:
```python
import math

import jax
import jax.numpy as jnp
from jax import lax
from jax.sharding import PartitionSpec as P

D = 4096
RANK = 4


noise_scale = 0.5


def laid_out(parts, dim):
    parts = jnp.moveaxis(parts, 0, dim)
    lengths = parts.shape
    return parts.reshape(*lengths[:dim], lengths[dim] * lengths[dim + 1], *lengths[dim + 2 :])


def copy_for_each(x, axis):
    count = lax.axis_size(axis)
    return lax.all_to_all(jnp.broadcast_to(x[None], (count, *x.shape)), axis, 0, 0, tiled=True)


def gather_directly(x, axis, dim):
    return laid_out(copy_for_each(x, axis), dim)


def taken_together(x, axis):
    return copy_for_each(x, axis).sum(axis=0)


def contract_members(left_rows, right_rows):
    return lax.dot_general(
        left_rows, right_rows, (((0,), (0,)), ((), ())), preferred_element_type=jnp.float32
    )


def local(tokens, weight, old_left, old_right, selected, shaping, new_left, new_right):
    groups = lax.axis_size("pop")
    picked = selected[0]
    count = picked.shape[0]
    factor = 1.0 / math.sqrt(D * RANK * count * groups)
    weights_here = shaping[0] * factor
    chosen_left = jnp.take(old_left, picked, axis=0)
    chosen_right = jnp.take(old_right, picked, axis=0)
    scaled_local = (chosen_left.astype(jnp.float32) * weights_here[:, None, None]).astype(
        jnp.bfloat16
    )
    scaled_left = gather_directly(scaled_local, "col", 2)
    every_left = lax.all_gather(scaled_left, "pop", axis=0, tiled=True)
    narrow_right = lax.all_to_all(chosen_right, "pop", split_axis=2, concat_axis=0, tiled=True)
    delta = contract_members(
        every_left.reshape(-1, D), narrow_right.reshape(-1, narrow_right.shape[2])
    )
    updated = (weight.astype(jnp.float32) + delta).astype(jnp.bfloat16)
    base = jnp.dot(
        tokens,
        lax.all_gather(updated, "pop", axis=1, tiled=True),
        preferred_element_type=jnp.float32,
    )
    members_here = new_left.shape[0]
    slab = new_left.shape[2]
    offset = lax.axis_index("col") * slab
    token_slab = lax.dynamic_slice_in_dim(tokens, offset, slab, 1).reshape(members_here, -1, slab)
    partial_proj = jnp.einsum(
        "mtd,mrd->mtr", token_slab, new_left, preferred_element_type=jnp.float32
    )
    proj = taken_together(partial_proj, "col").astype(jnp.bfloat16)
    side = jnp.einsum("mtr,mrh->mth", proj, new_right, preferred_element_type=jnp.float32).reshape(
        base.shape
    )
    pre = base + noise_scale / math.sqrt(D * RANK) * side
    return (updated, (jnp.maximum(pre, 0.0) ** 2).astype(jnp.bfloat16))


def solution(mesh):
    placed = (
        P("pop", None),
        P(None, ("col", "pop")),
        P("pop", None, "col"),
        P("pop", None, "col"),
        P("pop", None),
        P("pop", None),
        P("pop", None, "col"),
        P("pop", None, "col"),
    )
    return jax.shard_map(
        local,
        mesh=mesh,
        in_specs=placed,
        out_specs=(P(None, ("col", "pop")), P("pop", "col")),
        check_vma=False,
    )
```

profile of v0, /device:TPU:1, one launch (start us, length us, event | category | flops | bytes accessed | tf_op | source)
XLA Modules:
  0.0 255.4 jit_solution(2421390312344441921)
XLA Ops:
  7.2 0.0 copy-start
  7.2 0.0 all-gather.3.cloned.1.call-start
  7.2 0.7 fusion.7
  8.0 0.7 compare_and_fusion
  8.6 0.7 multiply_bitcast_fusion.1
  9.3 1.5 gather_fusion
  10.8 0.1 multiply_convert_fusion
  10.9 18.4 %all_to_all.25 = bf16[16,8,4,256]{3,1,2,0:T(8,128)(2,1)S(1)} all-to-all(bf16[16,8,4,256]{3,1,2,0:T(8,128)(2,1)S(1)} %broadcast_in_dim.35), channel_id=1, replica_groups=mesh['pop'=16,'col'=16] {'col'}, dimensions={0} | all-to-all | bytes 524288 | tf_op jit(solution)/shard_map/all_to_all | solution.py:23
  29.3 0.7 copy.63
  30.0 0.0 all-gather.3.cloned.1.call-update
  30.0 0.0 all-gather.5.cloned.1.call-start
  30.1 1.8 gather_fusion.1
  31.9 0.1 broadcast_select_fusion
  32.0 0.7 copy.57
  32.7 1.1 reshape.88
  33.8 20.4 %all_to_all.26 = bf16[16,2,1024]{2,1,0:T(2,128)(2,1)S(1)} all-to-all(bf16[16,2,1024]{2,1,0:T(2,128)(2,1)S(1)} %reshape.88), channel_id=1, replica_groups=mesh['pop'=16,'col'=16] {'pop'}, dimensions={0} | all-to-all | bytes 131072 | tf_op jit(solution)/shard_map/all_to_all | solution.py:53
  54.2 1.2 reshape.89
  55.4 0.5 copy.58
  56.0 52.5 %all-gather.3.cloned.1.call-done = bf16[128,4,4096]{2,0,1:T(8,128)(2,1)} async-done(((bf16[8,4,4096]{2,0,1:T(8,128)(2,1)}), bf16[128,4,4096]{2,0,1:T(8,128)(2,1)}) %all-gather.3.cloned.1.call-update) | async-done | bytes 4194320 | tf_op jit(solution)/shard_map/all_gather | solution.py:52
  108.5 7.4 %copy.56 = bf16[128,4,4096]{2,1,0:T(4,128)(2,1)} copy(bf16[128,4,4096]{2,0,1:T(8,128)(2,1)} %all-gather.3.cloned.1.call-done) | data formatting | bytes 8388608 | tf_op jit(solution)/shard_map/all_gather | solution.py:52
  115.9 0.0 copy-start.1
  115.9 7.0 %reshape.69 = bf16[512,4096]{1,0:T(8,128)(2,1)} reshape(bf16[128,4,4096]{2,1,0:T(4,128)(2,1)} %copy.56) | data formatting | bytes 8388608 | tf_op jit(solution)/shard_map/reshape | solution.py:55
  122.9 0.0 copy-start.2
  122.9 0.0 copy-done.1
  122.9 3.9 %fusion = bf16[4096,64]{0,1:T(8,128)(2,1)} fusion(bf16[512,4096]{1,0:T(8,128)(2,1)} %reshape.69, bf16[512,64]{1,0:T(8,128)(2,1)S(1)} %bitcast.41, bf16[4096,64]{0,1:T(8,128)(2,1)S(1)} %copy-done.1), kind=kOutput, calls=%fused_computation.3 | convolution fusion | flops 269221888 | bytes 5308416 | tf_op jit(solution)/shard_map/dot_general | solution.py:35
  126.8 0.0 all-gather.5.cloned.1.call-update
  126.8 0.0 copy-done.2
  126.8 1.3 fusion.4
  128.1 0.1 copy.59
  128.2 0.1 broadcast_in_dim.38
  128.3 14.1 %all_to_all.27 = f32[16,112,8,4]{1,2,3,0:T(8,128)S(1)} all-to-all(f32[16,112,8,4]{1,2,3,0:T(8,128)S(1)} %broadcast_in_dim.38), channel_id=1, replica_groups=mesh['pop'=16,'col'=16] {'col'}, dimensions={0} | all-to-all | bytes 458752 | tf_op jit(solution)/shard_map/all_to_all | solution.py:23
  142.4 0.2 copy.60
  142.6 0.0 copy-done
  142.6 2.6 %multiply_bitcast_fusion = f32[896,1024]{1,0:T(8,128)} fusion(bf16[112,8,4]{1,2,0:T(4,128)(2,1)S(1)} %copy.60, bf16[112,4,1024]{2,1,0:T(4,128)(2,1)S(1)} %copy-done), kind=kOutput, calls=%fused_computation.8 | convolution fusion | flops 8257536 | bytes 4594688 | tf_op jit(solution)/shard_map/mtr,mrh->mth/dot_general | solution.py:71
  145.1 5.0 %copy.61 = f32[896,1024]{0,1:T(8,128)} copy(f32[896,1024]{1,0:T(8,128)} %multiply_bitcast_fusion) | data formatting | bytes 7340032 | tf_op jit(solution)/shard_map/mul | solution.py:74
  150.1 81.9 %all-gather.5.cloned.1.call-done = bf16[4096,1024]{0,1:T(8,128)(2,1)} async-done(((bf16[4096,64]{0,1:T(8,128)(2,1)}), bf16[4096,1024]{0,1:T(8,128)(2,1)}) %all-gather.5.cloned.1.call-update) | async-done | bytes 8388624 | tf_op jit(solution)/shard_map/all_gather | solution.py:60
  232.1 14.0 %fusion.3 = bf16[896,1024]{0,1:T(8,128)(2,1)S(1)} fusion(f32[896,1024]{0,1:T(8,128)} %copy.61, bf16[4096,1024]{0,1:T(8,128)(2,1)} %all-gather.5.cloned.1.call-done, bf16[896,4096]{1,0:T(8,128)(2,1)} %param.8), kind=kOutput, calls=%fused_computation.7 | convolution fusion | flops 7519862784 | bytes 21233664 | tf_op jit(solution)/shard_map/dot_general | solution.py:58
  246.1 2.4 copy.62
  (3 shorter events, 0.1 us)
Async XLA Ops:
  7.2 135.4 %copy-start = (bf16[112,4,1024]{2,1,0:T(4,128)(2,1)S(1)}, bf16[112,4,1024]{2,1,0:T(4,128)(2,1)}, u32[]{:S(2)}) copy-start(bf16[112,4,1024]{2,1,0:T(4,128)(2,1)} %param.15) | copy-start | bytes 2752516
  7.2 101.3 %all-gather.3.cloned.1.call-start = ((), (), s32[]{:S(2)}) async-start(), calls=%async_computation.3 | async-start | bytes 4456448 | tf_op jit(solution)/shard_map/all_gather | solution.py:52
  30.0 202.1 %all-gather.5.cloned.1.call-start = ((), (), s32[]{:S(2)}) async-start(), calls=%async_computation.4 | async-start | bytes 8912896 | tf_op jit(solution)/shard_map/all_gather | solution.py:60
  115.9 7.0 %copy-start.1 = (bf16[4096,64]{0,1:T(8,128)(2,1)S(1)}, bf16[4096,64]{0,1:T(8,128)(2,1)}, u32[]{:S(2)}) copy-start(bf16[4096,64]{0,1:T(8,128)(2,1)} %param.9) | copy-start | bytes 1572868
  122.9 3.9 %copy-start.2 = (bf16[112,4,256]{2,1,0:T(4,128)(2,1)S(1)}, bf16[112,4,256]{2,1,0:T(4,128)(2,1)}, u32[]{:S(2)}) copy-start(bf16[112,4,256]{2,1,0:T(4,128)(2,1)} %param.14) | copy-start | bytes 688132
Sparse Core Ops, SparseCore 0:
  30.2 78.3 all-gather.2
  127.0 105.0 all-gather.4
where the time goes:
time: 256 us; the launch traced here: 255 us
  waiting for transfers between devices  135 us (53%)
  blocking collectives  52.9 us (21%)
  local copies, waits for them, and re-layouts  29.7 us (12%)
  matrix products  21.8 us (9%)
  between operations  14.1 us (6%)
    all_gather x1, waiting for transfers between devices, local(): lax.all_gather(updated, 'pop', axis=1, tiled=True)  81.9 us
    all_gather x1, waiting for transfers between devices, local(): every_left = lax.all_gather(scaled_left, 'pop', axis=0, tiled=True)  52.5 us
    all_to_all x2, blocking collectives, copy_for_each(): lax.all_to_all(jnp.broadcast_to(x[None], (count, *x.shape)), axis, 0, 0,...  32.5 us
    all_to_all x1, blocking collectives, local(): lax.all_to_all(chosen_right, 'pop', split_axis=2, concat_axis=0, tiled=True)  20.4 us
    dot_general x1, matrix products, local(): jnp.dot(tokens, lax.all_gather(updated, 'pop', axis=1, tiled=True), prefe...  14 us
    all_gather x1, local copies, waits for them, and re-layouts, local(): every_left = lax.all_gather(scaled_left, 'pop', axis=0, tiled=True)  7.37 us
    reshape x1, local copies, waits for them, and re-layouts, local(): every_left.reshape(-1, D)  7 us
  transfers between devices with their start and end apart: 2, of which 2 were waited for; matrix products, arithmetic and copies ran while one was open for 6% of the time, Pallas kernels for 0%

commit v1 on v0

v1 whole, which is shorter than its diff:
```python
import functools
import math

import jax
import jax.numpy as jnp
from jax import lax
from jax.experimental import pallas as pl
from jax.experimental.pallas import tpu as pltpu
from jax.sharding import PartitionSpec as P

MESH = pl.DeviceIdType.MESH
F32, BF16 = jnp.float32, jnp.bfloat16

D = 4096
RANK = 4
ROWS = 896
COLS = 1024
OWN = 64
MEM = 112
SEL = 8
SLAB = 256
CHUNKS = 8
LEN = D // CHUNKS
RCH = CHUNKS
NCH = CHUNKS + 1
noise_scale = 0.5
FACTOR = 1.0 / math.sqrt(D * RANK * SEL * 16)
SIDE = noise_scale / math.sqrt(D * RANK)


def nt(a, b):
    return lax.dot_general(a, b, (((1,), (1,)), ((), ())), preferred_element_type=F32)


def nn(a, b):
    return lax.dot_general(a, b, (((1,), (0,)), ((), ())), preferred_element_type=F32)


def kernel(
    tok_h, w_h, oldl_h, oldr_h, sel, shp, newl_h, newr_h,
    upd_h, act_h,
    tok, wall, rall, lall, trw, trr, oldl, oldr, newl, newr, nl, nr,
    acc, tacc, tb, cx, cz, rt, upd, outv,
    ld, st, ssw, sly, slz, slx, sls, spx,
    rp, rm, r2, tz, rz, dd, ly, lzp, lzm, lxp, lxm, lx2, dl, px,
):
    pop, col = lax.axis_index("pop"), lax.axis_index("col")
    y, zh, core = pop // 4, (pop // 2) % 2, pop % 2
    zlo, x = col // 4, col % 4
    z = zh * 4 + zlo

    def dev(y_, z_, core_, x_):
        return (y_ * 4 + (z_ // 4) * 2 + core_, (z_ % 4) * 4 + x_)

    yp, ym, yo = (y + 1) % 4, (y + 3) % 4, (y + 2) % 4
    xp, xm, xo = (x + 1) % 4, (x + 3) % 4, (x + 2) % 4
    Yp, Ym, Yo = dev(yp, z, core, x), dev(ym, z, core, x), dev(yo, z, core, x)
    Xp, Xm, Xo = dev(y, z, core, xp), dev(y, z, core, xm), dev(y, z, core, xo)

    def zdev(step):
        return dev(y, (z + step + 8) % 8, core, x)

    Zp1, Zm1, Zp2, Zm2 = zdev(1), zdev(-1), zdev(2), zdev(-2)
    Sib = dev(y, z, 1 - core, x)
    Zl = [dev(y, zh * 4 + (zlo + j) % 4, core, x) for j in (1, 2, 3)]

    def send(src, dst, ssem, rsem, to):
        pltpu.make_async_remote_copy(
            src_ref=src, dst_ref=dst, send_sem=ssem, recv_sem=rsem,
            device_id=to, device_id_type=MESH,
        ).start()

    def arrived(dst, rsem):
        pltpu.make_async_remote_copy(
            src_ref=dst, dst_ref=dst, send_sem=ssw.at[0], recv_sem=rsem,
            device_id=Sib, device_id_type=MESH,
        ).wait_recv()

    def sent(src, ssem):
        pltpu.make_async_remote_copy(
            src_ref=src, dst_ref=src, send_sem=ssem, recv_sem=rp.at[0, 0],
            device_id=Sib, device_id_type=MESH,
        ).wait_send()

    def piece(zh_, y_, k):
        if k == RCH:
            return rall.at[pl.ds(pl.multiple_of(((zh_ * 2 + core) * 4 + y_) * 32, 32), 32), :]
        return wall.at[zh_, pl.ds(pl.multiple_of((y_ * 2 + core) * OWN, OWN), OWN), k * LEN:(k + 1) * LEN]

    def transit(k):
        return trr if k == RCH else trw.at[k]

    def lpiece(z_, x_):
        c_ = (z_ % 4) * 4 + x_
        return lall.at[c_, pl.ds(pl.multiple_of(((z_ // 4) * 2 + core) * 128, 128), 128), :]

    mine = wall.at[zh, pl.ds(pl.multiple_of((y * 2 + core) * OWN, OWN), OWN), :]
    loads = [
        pltpu.make_async_copy(s, d, ld.at[i])
        for i, (s, d) in enumerate((
            (w_h, mine), (oldl_h, oldl), (oldr_h, oldr), (newl_h, newl), (newr_h, newr), (tok_h, tok),
        ))
    ]
    for cp in loads:
        cp.start()

    barrier = pltpu.get_barrier_semaphore()
    partners = [Yp, Ym, Yo, Xp, Xm, Xo, Zp1, Zm1, Zp2, Zm2, Sib] + Zl
    for to in partners:
        pl.semaphore_signal(barrier, inc=1, device_id=to, device_id_type=MESH)

    def rows_of(ref, ids, scales=None):
        parts = [ref[i].astype(F32) for i in ids]
        if scales is not None:
            parts = [p * s for p, s in zip(parts, scales)]
        return jnp.concatenate(parts, axis=0).astype(BF16)

    ids = [sel[0, j] for j in range(SEL)]
    loads[1].wait()
    lrow = pl.multiple_of((zh * 2 + core) * 128 + y * 32, 32)
    lall[col, pl.ds(lrow, 32), :] = rows_of(oldl, ids, [shp[0, j] * F32(FACTOR) for j in range(SEL)])
    loads[2].wait()
    v = rows_of(oldr, ids)
    rrow = pl.multiple_of(((zh * 2 + core) * 4 + y) * 32, 32)
    for b in range(8):
        h_, y_ = b % 2, b // 2
        rall[pl.ds(rrow, 32), h_ * 512 + y_ * 128:h_ * 512 + (y_ + 1) * 128] = v[:, b * 128:(b + 1) * 128]
    loads[0].wait()
    pl.semaphore_wait(barrier, len(partners))

    def start_left():
        src = lall.at[col, pl.ds(lrow, 32), :]
        for j, to in enumerate((Yp, Ym, Yo)):
            send(src, src, sly.at[j], ly.at[j], to)

    def own_y(k):
        src = piece(zh, y, k)
        send(src, src, ssw.at[k], rp.at[0, k], Yp)
        send(src, src, ssw.at[k], rm.at[0, k], Ym)
        send(src, src, ssw.at[k], dd.at[0, k], Sib)

    def own_z(k):
        send(piece(zh, y, k), transit(k), ssw.at[k], tz.at[k], Zp2 if k % 2 == 0 else Zm2)

    def pass_z(k):
        arrived(transit(k), tz.at[k])
        step = -2 if k % 2 == 0 else 2
        from_zh = ((z + step + 8) % 8) // 4
        send(transit(k), piece(from_zh, y, k), ssw.at[k], rz.at[k], Zp2 if k % 2 == 0 else Zm2)

    def other_y(k):
        src = piece(1 - zh, y, k)
        arrived(src, rz.at[k])
        send(src, src, ssw.at[k], rp.at[1, k], Yp)
        send(src, src, ssw.at[k], rm.at[1, k], Ym)
        send(src, src, ssw.at[k], dd.at[1, k], Sib)

    def got_p(s, k):
        h_ = zh if s == 0 else 1 - zh
        src = piece(h_, ym, k)
        arrived(src, rp.at[s, k])
        if k % 2 == 0:
            send(src, src, ssw.at[k], r2.at[s, k], Yp)
        send(src, src, ssw.at[k], dd.at[s, k], Sib)

    def got_m(s, k):
        h_ = zh if s == 0 else 1 - zh
        src = piece(h_, yp, k)
        arrived(src, rm.at[s, k])
        if k % 2 == 1:
            send(src, src, ssw.at[k], r2.at[s, k], Ym)
        send(src, src, ssw.at[k], dd.at[s, k], Sib)

    def got_2(s, k):
        h_ = zh if s == 0 else 1 - zh
        src = piece(h_, yo, k)
        arrived(src, r2.at[s, k])
        send(src, src, ssw.at[k], dd.at[s, k], Sib)

    def got_all(s, k):
        if k == RCH:
            arrived(rall.at[0:128, :], dd.at[s, k])
        else:
            h_ = zh if s == 0 else 1 - zh
            arrived(wall.at[h_, 0:256, k * LEN:(k + 1) * LEN], dd.at[s, k])

    def z_of(i):
        return z if i == 0 else ((z + 8 - i) % 8 if i <= 4 else (z + i - 4) % 8)

    def left_out(i):
        src = lpiece(z_of(i), x)
        send(src, src, slx, lxp.at[i], Xp)
        send(src, src, slx, lxm.at[i], Xm)
        send(src, src, sls, dl.at[(z_of(i) % 4) * 4 + x], Sib)

    def left_own():
        for j, y_ in enumerate((ym, yp, yo)):
            arrived(lall.at[col, pl.ds(pl.multiple_of((zh * 2 + core) * 128 + y_ * 32, 32), 32), :], ly.at[j])
        src = lpiece(z, x)
        send(src, src, slz.at[0], lzp.at[0], Zp1)
        send(src, src, slz.at[1], lzm.at[0], Zm1)
        left_out(0)

    def left_p(d):
        src = lpiece(z_of(d), x)
        arrived(src, lzp.at[d - 1])
        if d < 4:
            send(src, src, slz.at[1 + d], lzp.at[d], Zp1)
        left_out(d)

    def left_m(d):
        src = lpiece(z_of(4 + d), x)
        arrived(src, lzm.at[d - 1])
        if d < 3:
            send(src, src, slz.at[4 + d], lzm.at[d], Zm1)
        left_out(4 + d)

    def left_x(which, i):
        x_, sem = {"p": (xm, lxp), "m": (xp, lxm), "2": (xo, lx2)}[which]
        src = lpiece(z_of(i), x_)
        arrived(src, sem.at[i])
        if which == "p" and i % 2 == 0:
            send(src, src, slx, lx2.at[i], Xp)
        if which == "m" and i % 2 == 1:
            send(src, src, slx, lx2.at[i], Xm)
        send(src, src, sls, dl.at[(z_of(i) % 4) * 4 + x_], Sib)

    def build_new():
        nl[448:512, :] = jnp.zeros((64, SLAB), BF16)
        for h_ in range(2):
            nr[h_, 448:512, :] = jnp.zeros((64, 512), BF16)
        loads[3].wait()
        loads[4].wait()

        def body(i, _):
            at = pl.ds(pl.multiple_of(i * 32, 32), 32)
            nl[at, :] = rows_of(newl, [i * 8 + j for j in range(8)])
            v = rows_of(newr, [i * 8 + j for j in range(8)])
            for b in range(8):
                nr[b % 2, at, (b // 2) * 128:(b // 2 + 1) * 128] = v[:, b * 128:(b + 1) * 128]
            return 0

        lax.fori_loop(0, MEM // 8, body, 0)

    def own_member(n):
        r = lax.broadcasted_iota(jnp.int32, (n, 128), 0)
        c = lax.broadcasted_iota(jnp.int32, (n, 128), 1)
        return (r >> 3) == (c >> 2)

    def proj_part():
        loads[5].wait()
        lanes = pl.ds(pl.multiple_of(col * SLAB, SLAB), SLAB)
        for g in range(4):
            n = 256 if g < 3 else 128
            part = nt(tok[256 * g:256 * g + n, lanes], nl[128 * g:128 * (g + 1), :])
            part = jnp.where(own_member(n), part, 0.0)
            cx[x, :, 128 * g:128 * (g + 1)] = part.reshape(n // 8, 8, 128).sum(axis=0)
        src = cx.at[x]
        for j, to in enumerate((Xp, Xm, Xo)):
            send(src, src, spx.at[j], px.at[0], to)

    def proj_x():
        arrived(cx.at[0:3], px.at[0])
        cz[zlo] = (cx[0] + cx[1]) + (cx[2] + cx[3])
        src = cz.at[zlo]
        for j, to in enumerate(Zl):
            send(src, src, spx.at[3 + j], px.at[1], to)

    def proj_z():
        arrived(cz.at[0:3], px.at[1])
        proj = ((cz[0] + cz[1]) + (cz[2] + cz[3])).astype(BF16).astype(F32)
        for g in range(4):
            n = 256 if g < 3 else 128
            wide = jnp.broadcast_to(proj[:, 128 * g:128 * (g + 1)][None], (n // 8, 8, 128)).reshape(n, 128)
            wide = jnp.where(own_member(n), wide, 0.0).astype(BF16)
            for h_ in range(2):
                acc[h_, 256 * g:256 * g + n, :] = nn(wide, nr[h_, 128 * g:128 * (g + 1), :]) * SIDE

    def main_dot(s, k):
        h_ = zh if s == 0 else 1 - zh

        def body(n, _):
            at = pl.ds(pl.multiple_of(n * 256, 256), 256)
            acc[h_, :, at] += nt(tok[:, k * LEN:(k + 1) * LEN], wall[h_, at, k * LEN:(k + 1) * LEN])
            return 0

        lax.fori_loop(0, 2, body, 0)

    def t_dot(x_, first):
        for zlo_ in range(4):
            c = zlo_ * 4 + x_
            arrived(lall.at[c, 0:256, :], dl.at[c])

        def body(zlo_, _):
            c = zlo_ * 4 + x_
            part = nt(tok[:, pl.ds(pl.multiple_of(c * SLAB, SLAB), SLAB)], lall[c])
            tacc[...] += part
            return 0

        if first:
            tacc[...] = jnp.zeros_like(tacc)
        lax.fori_loop(0, 4, body, 0)

    def make_rt():
        base = pl.multiple_of(zh * 512 + y * 128, 128)
        rt[...] = rall[:, pl.ds(base, 128)].astype(F32).T.astype(BF16)

    def update(x_):
        def body(zlo_, _):
            c = zlo_ * 4 + x_
            at = pl.ds(pl.multiple_of(c * SLAB, SLAB), SLAB)
            own = wall[zh, pl.ds(pl.multiple_of((y * 2 + core) * OWN, OWN), OWN), at]
            delta = nn(rt[pl.ds(pl.multiple_of(core * OWN, OWN), OWN), :], lall[c])
            upd[:, at] = (own.astype(F32) + delta).astype(BF16)
            return 0

        lax.fori_loop(0, 4, body, 0)

    def t_right():
        tb[...] = tacc[...].astype(BF16)

        def body(i, _):
            h_, at = i // 2, pl.ds(pl.multiple_of((i % 2) * 256, 256), 256)
            acc[h_, :, at] += nn(tb[...], rall[:, pl.ds(pl.multiple_of(i * 256, 256), 256)])
            return 0

        lax.fori_loop(0, 4, body, 0)

    def out_copy(s, y_):
        h_ = zh if s == 0 else 1 - zh
        at = pl.ds(pl.multiple_of((2 * y_ + h_) * 128, 128), 128)
        return pltpu.make_async_copy(outv.at[:, at], act_h.at[:, at], st.at[s * 4 + y_])

    def finish(s):
        h_ = zh if s == 0 else 1 - zh
        for y_ in range(4):
            at = pl.ds(pl.multiple_of((2 * y_ + h_) * 128, 128), 128)
            pre = jnp.maximum(acc[h_, :, y_ * 128:(y_ + 1) * 128], 0.0)
            outv[:, at] = (pre * pre).astype(BF16)
            out_copy(s, y_).start()

    def store_update():
        pltpu.make_async_copy(upd, upd_h, st.at[8]).start()

    order = [RCH] + list(range(CHUNKS))
    events = [(0.0, start_left)]
    for i, k in enumerate(order):
        events.append((0.1 + 0.001 * i, functools.partial(own_y, k)))
        events.append((0.1005 + 0.001 * i if i < 4 else 3.0 + 2.0 * (i // 2), functools.partial(own_z, k)))
        for s, base in ((0, 3.0), (1, 0.0)):
            t = 3.2 + 1.5 * i if s == 0 else 20.5 + 2.0 * i
            events.append((t, functools.partial(got_p, s, k)))
            events.append((t + 0.001, functools.partial(got_m, s, k)))
            t2 = 15.0 + 0.7 * i if s == 0 else 25.0 + 1.8 * i
            events.append((t2, functools.partial(got_2, s, k)))
            events.append((t2 + 2.0, functools.partial(got_all, s, k)))
            if k != RCH:
                events.append((t2 + 2.01, functools.partial(main_dot, s, k)))
        pair = i // 2
        events.append((5.0 + 4.0 * pair, functools.partial(pass_z, k)))
        events.append((9.5 + 4.5 * pair, functools.partial(other_y, k)))
    events += [
        (1.0, build_new), (2.0, proj_part), (3.5, left_own), (6.0, proj_x), (9.0, proj_z),
    ]
    for d in range(1, 5):
        events.append((3.5 + 4.0 * d, functools.partial(left_p, d)))
        if d < 4:
            events.append((3.51 + 4.0 * d, functools.partial(left_m, d)))
    for i in range(8):
        step = 0 if i == 0 else (i if i <= 4 else i - 4)
        t = 7.5 + 4.0 * step
        events.append((t, functools.partial(left_x, "p", i)))
        events.append((t + 0.001, functools.partial(left_x, "m", i)))
        events.append((t + 4.0, functools.partial(left_x, "2", i)))
    events += [
        (28.1, functools.partial(t_dot, x, True)),
        (28.2, functools.partial(t_dot, xm, False)),
        (28.3, functools.partial(t_dot, xp, False)),
        (30.1, functools.partial(t_dot, xo, False)),
        (30.2, t_right),
        (32.9, make_rt),
        (33.0, functools.partial(update, x)),
        (33.1, functools.partial(update, xm)),
        (33.2, functools.partial(update, xp)),
        (33.3, functools.partial(update, xo)),
        (33.4, store_update),
        (33.5, functools.partial(finish, 0)),
        (90.0, functools.partial(finish, 1)),
    ]
    for _, event in sorted(events, key=lambda e: e[0]):
        event()

    for k in range(NCH):
        sent(wall.at[:, :, 0:LEN], ssw.at[k])
    for j in range(3):
        sent(lall.at[0, 0:32, :], sly.at[j])
    for j in range(7):
        sent(lall.at[0, 0:128, :], slz.at[j])
    sent(lall.at[0:6], slx)
    sent(lall.at[0:8], sls)
    for j in range(6):
        sent(cx.at[0], spx.at[j])
    for s in range(2):
        for y_ in range(4):
            out_copy(s, y_).wait()
    pltpu.make_async_copy(upd, upd_h, st.at[8]).wait()


def local(tokens, weight, old_left, old_right, selected, shaping, new_left, new_right):
    dma = pltpu.SemaphoreType.DMA
    anywhere = pl.BlockSpec(memory_space=pl.ANY)
    scalars = pl.BlockSpec(memory_space=pltpu.SMEM)
    upd, act = pl.pallas_call(
        kernel,
        out_shape=(
            jax.ShapeDtypeStruct((OWN, D), BF16),
            jax.ShapeDtypeStruct((ROWS, COLS), BF16),
        ),
        in_specs=[anywhere] * 4 + [scalars] * 2 + [anywhere] * 2,
        out_specs=(anywhere, anywhere),
        scratch_shapes=[
            pltpu.VMEM((ROWS, D), BF16),
            pltpu.VMEM((2, 512, D), BF16),
            pltpu.VMEM((512, COLS), BF16),
            pltpu.VMEM((16, 512, SLAB), BF16),
            pltpu.VMEM((CHUNKS, OWN, LEN), BF16),
            pltpu.VMEM((32, COLS), BF16),
            pltpu.VMEM((MEM, RANK, SLAB), BF16),
            pltpu.VMEM((MEM, RANK, COLS), BF16),
            pltpu.VMEM((MEM, RANK, SLAB), BF16),
            pltpu.VMEM((MEM, RANK, COLS), BF16),
            pltpu.VMEM((512, SLAB), BF16),
            pltpu.VMEM((2, 512, 512), BF16),
            pltpu.VMEM((2, ROWS, 512), F32),
            pltpu.VMEM((ROWS, 512), F32),
            pltpu.VMEM((ROWS, 512), BF16),
            pltpu.VMEM((4, 8, 512), F32),
            pltpu.VMEM((4, 8, 512), F32),
            pltpu.VMEM((128, 512), BF16),
            pltpu.VMEM((OWN, D), BF16),
            pltpu.VMEM((ROWS, COLS), BF16),
            dma((6,)), dma((9,)), dma((NCH,)), dma((3,)), dma((7,)), dma(()), dma(()), dma((6,)),
            dma((2, NCH)), dma((2, NCH)), dma((2, NCH)), dma((NCH,)), dma((NCH,)), dma((2, NCH)),
            dma((3,)), dma((4,)), dma((3,)), dma((8,)), dma((8,)), dma((8,)), dma((16,)), dma((2,)),
        ],
        compiler_params=pltpu.CompilerParams(
            collective_id=0, has_side_effects=True, vmem_limit_bytes=56 * 1024 * 1024
        ),
        name="gather_and_project",
    )(tokens, weight.T, old_left, old_right, selected, shaping, new_left, new_right)
    return (upd.T, act)


def solution(mesh):
    placed = (
        P("pop", None),
        P(None, ("col", "pop")),
        P("pop", None, "col"),
        P("pop", None, "col"),
        P("pop", None),
        P("pop", None),
        P("pop", None, "col"),
        P("pop", None, "col"),
    )
    return jax.shard_map(
        local,
        mesh=mesh,
        in_specs=placed,
        out_specs=(P(None, ("col", "pop")), P("pop", "col")),
        check_vma=False,
    )
```

time: 256 us -> 85.8 us (0.34)
  waiting for transfers between devices: 135 us -> 0 us
  Pallas kernels: 0 us -> 80.3 us
  blocking collectives: 52.9 us -> 0 us
  local copies, waits for them, and re-layouts: 29.7 us -> 4.74 us
  matrix products: 21.8 us -> 0 us
  between operations: 14.1 us -> 0.64 us
    all_gather x2 -> x0, waiting for transfers between devices: 134 us -> none  [the longest x1 81.9 us: local(): lax.all_gather(updated, 'pop', axis=1, tiled=True)]
    pallas_call x0 -> x1, Pallas kernels: none -> 80.3 us  [local(): pl.pallas_call(kernel, out_shape=(jax.ShapeDtypeStruct((OWN, D), BF16), j...]
    all_to_all x3 -> x0, blocking collectives: 52.9 us -> none  [the longest x2 32.5 us: copy_for_each(): lax.all_to_all(jnp.broadcast_to(x[None], (count, *x.shape)), axis, 0, 0,...]
    dot_general x4 -> x0, matrix products: 21.8 us -> none  [the longest x1 14 us: local(): jnp.dot(tokens, lax.all_gather(updated, 'pop', axis=1, tiled=True), prefe...]
    reshape x2 -> x0, local copies, waits for them, and re-layouts: 7.72 us -> none  [the longest x1 7 us: local(): every_left.reshape(-1, D)]
    all_gather x1 -> x0, local copies, waits for them, and re-layouts: 7.37 us -> none  [local(): every_left = lax.all_gather(scaled_left, 'pop', axis=0, tiled=True)]
    mul x1 -> x0, local copies, waits for them, and re-layouts: 5 us -> none  [local(): pre = base + noise_scale / math.sqrt(D * RANK) * side]
    gather x2 -> x0, local copies, waits for them, and re-layouts: 3.3 us -> none  [the longest x1 1.79 us: local(): chosen_right = jnp.take(old_right, picked, axis=0)]
  transfers between devices with their start and end apart: 2 -> 0, of which waited for: 2 -> 0; matrix products, arithmetic and copies ran while one was open for 6% -> 0% of each run, Pallas kernels for 0% -> 0%
where the time goes in v1:
time: 85.8 us; the launch traced here: 85.7 us
  Pallas kernels  80.3 us (94%)
  local copies, waits for them, and re-layouts  4.74 us (6%)
    pallas_call x1, Pallas kernels, local(): pl.pallas_call(kernel, out_shape=(jax.ShapeDtypeStruct((OWN, D), BF16), j...  80.3 us
    unnamed x2, local copies, waits for them, and re-layouts  4.74 us

profile of v1, /device:TPU:1, one launch (start us, length us, event | category | flops | bytes accessed | tf_op | source)
XLA Modules:
  0.0 85.7 jit_solution(13752579857670849195)
XLA Ops:
  0.6 80.3 %gather_and_project.1 = (bf16[64,4096]{1,0:T(8,128)(2,1)}, bf16[896,1024]{1,0:T(8,128)(2,1)}) custom-call(bf16[896,4096]{1,0:T(8,128)(2,1)} %tok_h.1, bf16[64,4096]{1,0:T(8,128)(2,1)} %bitcast.3, bf16[112,4,256]{2,1,0:T(4,128)(2,1)} %oldl_h.1, bf16[112,4,1024]{2,1,0:T(4,128)(2,1)} %oldr_h.1, s32[1,8]{1,0:T(1,128)} %sel.1, f32[1,8]{1,0:T(1,128)} %shp.1, ...), custom_call_target="tpu_custom_call" | custom-call | tf_op jit(solution)/shard_map/gather_and_project/pallas_call | solution.py:413
  80.9 1.9 %copy.12 = bf16[4096,64]{0,1:T(8,128)(2,1)} copy(bf16[4096,64]{0,1:T(8,128)(2,1)} %bitcast.2) | data formatting | bytes 1048576
  82.8 2.9 %copy.13 = bf16[896,1024]{1,0:T(8,128)(2,1)} copy(bf16[896,1024]{1,0:T(8,128)(2,1)} %get-tuple-element.9) | data formatting | bytes 3670016

commit v2 on v1

--- a/solution.py
+++ b/solution.py
@@ -24,10 +24,41 @@
 RCH = CHUNKS
 NCH = CHUNKS + 1
 noise_scale = 0.5
+ORDER = (
+    ("start_left",), ("own_y", 0), ("own_y", 1), ("own_y", 2), ("own_y", 3), ("pick_right",), ("own_y", 8),
+    ("own_y", 4), ("own_y", 5), ("own_y", 6), ("own_y", 7), ("build_new",), ("proj_part",), ("own_z", 0),
+    ("own_z", 1), ("own_z", 2), ("own_z", 3), ("got_m", 0, 0), ("left_own",), ("proj_x",), ("got_p", 0, 0),
+    ("got_m", 0, 1), ("got_p", 0, 1), ("own_z", 8), ("own_z", 4), ("got_m", 0, 2), ("pass_z", 0), ("pass_z", 1),
+    ("got_p", 0, 2), ("got_m", 0, 3), ("got_p", 0, 3), ("got_m", 0, 8), ("pass_z", 2), ("pass_z", 3),
+    ("left_x", "m", 0), ("left_x", "p", 0), ("left_p", 1), ("left_m", 1), ("got_p", 0, 8), ("proj_z",),
+    ("got_p", 0, 4), ("got_m", 0, 4), ("got_m", 0, 5), ("got_p", 0, 5), ("got_m", 0, 6), ("pass_z", 4),
+    ("pass_z", 8), ("got_p", 0, 6), ("got_m", 0, 7), ("left_x", "2", 0), ("left_x", "m", 1), ("got_p", 0, 7),
+    ("got_2", 0, 1), ("left_x", "p", 1), ("other_y", 0), ("other_y", 1), ("left_x", "m", 5), ("got_2", 0, 0),
+    ("got_2", 0, 3), ("left_x", "p", 5), ("got_2", 0, 2), ("own_z", 5), ("own_z", 6), ("got_2", 0, 8),
+    ("other_y", 2), ("other_y", 3), ("got_2", 0, 4), ("left_p", 2), ("left_m", 2), ("got_2", 0, 5),
+    ("main_dot", 0, 0, 1), ("left_x", "2", 1), ("got_2", 0, 6), ("main_dot", 0, 2, 3), ("left_x", "2", 5),
+    ("got_2", 0, 7), ("own_z", 7), ("got_p", 1, 0), ("got_r", 0), ("got_m", 1, 0), ("other_y", 4), ("other_y", 8),
+    ("main_dot", 0, 4, 5), ("got_m", 1, 1), ("got_p", 1, 1), ("got_p", 1, 2), ("left_x", "m", 2), ("left_x", "p", 2),
+    ("got_m", 1, 2), ("main_dot", 0, 6, 7), ("left_m", 3), ("left_p", 3), ("left_x", "m", 6), ("left_x", "p", 6),
+    ("got_m", 1, 3), ("pass_z", 5), ("pass_z", 6), ("got_p", 1, 3), ("got_2", 1, 0), ("got_m", 1, 4),
+    ("got_p", 1, 4), ("got_m", 1, 8), ("pass_z", 7), ("left_x", "2", 2), ("got_p", 1, 8), ("got_2", 1, 1),
+    ("got_2", 1, 2), ("left_x", "m", 7), ("left_p", 4), ("left_x", "p", 7), ("got_2", 1, 3), ("left_x", "m", 3),
+    ("left_x", "p", 3), ("main_dot", 1, 0, 1), ("other_y", 5), ("left_x", "2", 6), ("got_2", 1, 8), ("got_2", 1, 4),
+    ("t_dot", 0), ("other_y", 6), ("main_dot", 1, 2, 3), ("other_y", 7), ("left_x", "2", 7), ("left_x", "p", 4),
+    ("left_x", "m", 4), ("got_r", 1), ("make_rt",), ("update", 0), ("left_x", "2", 3), ("got_m", 1, 5),
+    ("got_p", 1, 5), ("t_dot", 1), ("got_m", 1, 6), ("got_p", 1, 6), ("t_dot", 2), ("left_x", "2", 4),
+    ("got_m", 1, 7), ("got_p", 1, 7), ("update", 1), ("update", 2), ("got_2", 1, 5), ("t_dot", 3), ("got_2", 1, 6),
+    ("t_right", 0), ("t_right", 1), ("got_2", 1, 7), ("update", 3), ("main_dot", 1, 4, 5), ("finish", 0),
+    ("main_dot", 1, 6), ("main_dot", 1, 7), ("finish", 1),
+)
 FACTOR = 1.0 / math.sqrt(D * RANK * SEL * 16)
 SIDE = noise_scale / math.sqrt(D * RANK)
 
 
+def going_up(k):
+    return k % 2 == 0 and k != RCH
+
+
 def nt(a, b):
     return lax.dot_general(a, b, (((1,), (1,)), ((), ())), preferred_element_type=F32)
 
@@ -38,10 +69,10 @@
 
 def kernel(
     tok_h, w_h, oldl_h, oldr_h, sel, shp, newl_h, newr_h,
-    upd_h, act_h,
+    upd, outv,
     tok, wall, rall, lall, trw, trr, oldl, oldr, newl, newr, nl, nr,
-    acc, tacc, tb, cx, cz, rt, upd, outv,
-    ld, st, ssw, sly, slz, slx, sls, spx,
+    acc, tacc, tb, cx, cz, rt,
+    ld, ssw, sly, slz, slx, sls, spx,
     rp, rm, r2, tz, rz, dd, ly, lzp, lzm, lxp, lxm, lx2, dl, px,
 ):
     pop, col = lax.axis_index("pop"), lax.axis_index("col")
@@ -101,8 +132,8 @@
             (w_h, mine), (oldl_h, oldl), (oldr_h, oldr), (newl_h, newl), (newr_h, newr), (tok_h, tok),
         ))
     ]
-    for cp in loads:
-        cp.start()
+    for i in (1, 0, 2, 5, 3, 4):
+        loads[i].start()
 
     barrier = pltpu.get_barrier_semaphore()
     partners = [Yp, Ym, Yo, Xp, Xm, Xo, Zp1, Zm1, Zp2, Zm2, Sib] + Zl
@@ -119,12 +150,6 @@
     loads[1].wait()
     lrow = pl.multiple_of((zh * 2 + core) * 128 + y * 32, 32)
     lall[col, pl.ds(lrow, 32), :] = rows_of(oldl, ids, [shp[0, j] * F32(FACTOR) for j in range(SEL)])
-    loads[2].wait()
-    v = rows_of(oldr, ids)
-    rrow = pl.multiple_of(((zh * 2 + core) * 4 + y) * 32, 32)
-    for b in range(8):
-        h_, y_ = b % 2, b // 2
-        rall[pl.ds(rrow, 32), h_ * 512 + y_ * 128:h_ * 512 + (y_ + 1) * 128] = v[:, b * 128:(b + 1) * 128]
     loads[0].wait()
     pl.semaphore_wait(barrier, len(partners))
 
@@ -140,13 +165,13 @@
         send(src, src, ssw.at[k], dd.at[0, k], Sib)
 
     def own_z(k):
-        send(piece(zh, y, k), transit(k), ssw.at[k], tz.at[k], Zp2 if k % 2 == 0 else Zm2)
+        send(piece(zh, y, k), transit(k), ssw.at[k], tz.at[k], Zp2 if going_up(k) else Zm2)
 
     def pass_z(k):
         arrived(transit(k), tz.at[k])
-        step = -2 if k % 2 == 0 else 2
+        step = -2 if going_up(k) else 2
         from_zh = ((z + step + 8) % 8) // 4
-        send(transit(k), piece(from_zh, y, k), ssw.at[k], rz.at[k], Zp2 if k % 2 == 0 else Zm2)
+        send(transit(k), piece(from_zh, y, k), ssw.at[k], rz.at[k], Zp2 if going_up(k) else Zm2)
 
     def other_y(k):
         src = piece(1 - zh, y, k)
@@ -159,7 +184,7 @@
         h_ = zh if s == 0 else 1 - zh
         src = piece(h_, ym, k)
         arrived(src, rp.at[s, k])
-        if k % 2 == 0:
+        if going_up(k):
             send(src, src, ssw.at[k], r2.at[s, k], Yp)
         send(src, src, ssw.at[k], dd.at[s, k], Sib)
 
@@ -167,7 +192,7 @@
         h_ = zh if s == 0 else 1 - zh
         src = piece(h_, yp, k)
         arrived(src, rm.at[s, k])
-        if k % 2 == 1:
+        if not going_up(k):
             send(src, src, ssw.at[k], r2.at[s, k], Ym)
         send(src, src, ssw.at[k], dd.at[s, k], Sib)
 
@@ -177,12 +202,8 @@
         arrived(src, r2.at[s, k])
         send(src, src, ssw.at[k], dd.at[s, k], Sib)
 
-    def got_all(s, k):
-        if k == RCH:
-            arrived(rall.at[0:128, :], dd.at[s, k])
-        else:
-            h_ = zh if s == 0 else 1 - zh
-            arrived(wall.at[h_, 0:256, k * LEN:(k + 1) * LEN], dd.at[s, k])
+    def got_r(s):
+        arrived(rall.at[0:128, :], dd.at[s, RCH])
 
     def z_of(i):
         return z if i == 0 else ((z + 8 - i) % 8 if i <= 4 else (z + i - 4) % 8)
@@ -224,6 +245,14 @@
         if which == "m" and i % 2 == 1:
             send(src, src, slx, lx2.at[i], Xm)
         send(src, src, sls, dl.at[(z_of(i) % 4) * 4 + x_], Sib)
+
+    def pick_right():
+        loads[2].wait()
+        v = rows_of(oldr, ids)
+        rrow = pl.multiple_of(((zh * 2 + core) * 4 + y) * 32, 32)
+        for b in range(8):
+            h_, y_ = b % 2, b // 2
+            rall[pl.ds(rrow, 32), h_ * 512 + y_ * 128:h_ * 512 + (y_ + 1) * 128] = v[:, b * 128:(b + 1) * 128]
 
     def build_new():
         nl[448:512, :] = jnp.zeros((64, SLAB), BF16)
@@ -276,60 +305,43 @@
             for h_ in range(2):
                 acc[h_, 256 * g:256 * g + n, :] = nn(wide, nr[h_, 128 * g:128 * (g + 1), :]) * SIDE
 
-    def main_dot(s, k):
+    def main_dot(s, *ks):
         h_ = zh if s == 0 else 1 - zh
-
-        def body(n, _):
-            at = pl.ds(pl.multiple_of(n * 256, 256), 256)
-            acc[h_, :, at] += nt(tok[:, k * LEN:(k + 1) * LEN], wall[h_, at, k * LEN:(k + 1) * LEN])
-            return 0
-
-        lax.fori_loop(0, 2, body, 0)
-
-    def t_dot(x_, first):
-        for zlo_ in range(4):
-            c = zlo_ * 4 + x_
+        for k in ks:
+            arrived(wall.at[h_, 0:256, k * LEN:(k + 1) * LEN], dd.at[s, k])
+        deep = slice(ks[0] * LEN, (ks[-1] + 1) * LEN)
+        for n in range(2):
+            at = slice(n * 256, (n + 1) * 256)
+            acc[h_, :, at] += nt(tok[:, deep], wall[h_, at, deep])
+
+    xs = (x, xm, xp, xo)
+
+    def slab(c):
+        return pl.ds(pl.multiple_of(c * SLAB, SLAB), SLAB)
+
+    def t_dot(j):
+        cs = [zlo_ * 4 + xs[j] for zlo_ in range(4)]
+        for c in cs:
             arrived(lall.at[c, 0:256, :], dl.at[c])
-
-        def body(zlo_, _):
-            c = zlo_ * 4 + x_
-            part = nt(tok[:, pl.ds(pl.multiple_of(c * SLAB, SLAB), SLAB)], lall[c])
-            tacc[...] += part
-            return 0
-
-        if first:
-            tacc[...] = jnp.zeros_like(tacc)
-        lax.fori_loop(0, 4, body, 0)
+        part = sum(nt(tok[:, slab(c)], lall[c]) for c in cs)
+        tacc[...] = part if j == 0 else tacc[...] + part
 
     def make_rt():
         base = pl.multiple_of(zh * 512 + y * 128, 128)
         rt[...] = rall[:, pl.ds(base, 128)].astype(F32).T.astype(BF16)
 
-    def update(x_):
-        def body(zlo_, _):
-            c = zlo_ * 4 + x_
-            at = pl.ds(pl.multiple_of(c * SLAB, SLAB), SLAB)
-            own = wall[zh, pl.ds(pl.multiple_of((y * 2 + core) * OWN, OWN), OWN), at]
-            delta = nn(rt[pl.ds(pl.multiple_of(core * OWN, OWN), OWN), :], lall[c])
-            upd[:, at] = (own.astype(F32) + delta).astype(BF16)
-            return 0
-
-        lax.fori_loop(0, 4, body, 0)
-
-    def t_right():
-        tb[...] = tacc[...].astype(BF16)
-
-        def body(i, _):
-            h_, at = i // 2, pl.ds(pl.multiple_of((i % 2) * 256, 256), 256)
-            acc[h_, :, at] += nn(tb[...], rall[:, pl.ds(pl.multiple_of(i * 256, 256), 256)])
-            return 0
-
-        lax.fori_loop(0, 4, body, 0)
-
-    def out_copy(s, y_):
-        h_ = zh if s == 0 else 1 - zh
-        at = pl.ds(pl.multiple_of((2 * y_ + h_) * 128, 128), 128)
-        return pltpu.make_async_copy(outv.at[:, at], act_h.at[:, at], st.at[s * 4 + y_])
+    def update(j):
+        left = rt[pl.ds(pl.multiple_of(core * OWN, OWN), OWN), :]
+        for c in [zlo_ * 4 + xs[j] for zlo_ in range(4)]:
+            own = wall[zh, pl.ds(pl.multiple_of((y * 2 + core) * OWN, OWN), OWN), slab(c)]
+            upd[:, slab(c)] = (own.astype(F32) + nn(left, lall[c])).astype(BF16)
+
+    def t_right(h_):
+        if h_ == 0:
+            tb[...] = tacc[...].astype(BF16)
+        for n in range(2):
+            at = slice(n * 256, (n + 1) * 256)
+            acc[h_, :, at] += nn(tb[...], rall[:, h_ * 512 + n * 256:h_ * 512 + (n + 1) * 256])
 
     def finish(s):
         h_ = zh if s == 0 else 1 - zh
@@ -337,58 +349,13 @@
             at = pl.ds(pl.multiple_of((2 * y_ + h_) * 128, 128), 128)
             pre = jnp.maximum(acc[h_, :, y_ * 128:(y_ + 1) * 128], 0.0)
             outv[:, at] = (pre * pre).astype(BF16)
-            out_copy(s, y_).start()
-
-    def store_update():
-        pltpu.make_async_copy(upd, upd_h, st.at[8]).start()
-
-    order = [RCH] + list(range(CHUNKS))
-    events = [(0.0, start_left)]
-    for i, k in enumerate(order):
-        events.append((0.1 + 0.001 * i, functools.partial(own_y, k)))
-        events.append((0.1005 + 0.001 * i if i < 4 else 3.0 + 2.0 * (i // 2), functools.partial(own_z, k)))
-        for s, base in ((0, 3.0), (1, 0.0)):
-            t = 3.2 + 1.5 * i if s == 0 else 20.5 + 2.0 * i
-            events.append((t, functools.partial(got_p, s, k)))
-            events.append((t + 0.001, functools.partial(got_m, s, k)))
-            t2 = 15.0 + 0.7 * i if s == 0 else 25.0 + 1.8 * i
-            events.append((t2, functools.partial(got_2, s, k)))
-            events.append((t2 + 2.0, functools.partial(got_all, s, k)))
-            if k != RCH:
-                events.append((t2 + 2.01, functools.partial(main_dot, s, k)))
-        pair = i // 2
-        events.append((5.0 + 4.0 * pair, functools.partial(pass_z, k)))
-        events.append((9.5 + 4.5 * pair, functools.partial(other_y, k)))
-    events += [
-        (1.0, build_new), (2.0, proj_part), (3.5, left_own), (6.0, proj_x), (9.0, proj_z),
-    ]
-    for d in range(1, 5):
-        events.append((3.5 + 4.0 * d, functools.partial(left_p, d)))
-        if d < 4:
-            events.append((3.51 + 4.0 * d, functools.partial(left_m, d)))
-    for i in range(8):
-        step = 0 if i == 0 else (i if i <= 4 else i - 4)
-        t = 7.5 + 4.0 * step
-        events.append((t, functools.partial(left_x, "p", i)))
-        events.append((t + 0.001, functools.partial(left_x, "m", i)))
-        events.append((t + 4.0, functools.partial(left_x, "2", i)))
-    events += [
-        (28.1, functools.partial(t_dot, x, True)),
-        (28.2, functools.partial(t_dot, xm, False)),
-        (28.3, functools.partial(t_dot, xp, False)),
-        (30.1, functools.partial(t_dot, xo, False)),
-        (30.2, t_right),
-        (32.9, make_rt),
-        (33.0, functools.partial(update, x)),
-        (33.1, functools.partial(update, xm)),
-        (33.2, functools.partial(update, xp)),
-        (33.3, functools.partial(update, xo)),
-        (33.4, store_update),
-        (33.5, functools.partial(finish, 0)),
-        (90.0, functools.partial(finish, 1)),
-    ]
-    for _, event in sorted(events, key=lambda e: e[0]):
-        event()
+
+    steps = {f.__name__: f for f in (
+        start_left, own_y, own_z, pass_z, other_y, got_p, got_m, got_2, got_r, left_own, left_p, left_m, left_x,
+        pick_right, build_new, proj_part, proj_x, proj_z, main_dot, t_dot, make_rt, update, t_right, finish,
+    )}
+    for name, *rest in ORDER:
+        steps[name](*rest)
 
     for k in range(NCH):
         sent(wall.at[:, :, 0:LEN], ssw.at[k])
@@ -400,10 +367,6 @@
     sent(lall.at[0:8], sls)
     for j in range(6):
         sent(cx.at[0], spx.at[j])
-    for s in range(2):
-        for y_ in range(4):
-            out_copy(s, y_).wait()
-    pltpu.make_async_copy(upd, upd_h, st.at[8]).wait()
 
 
 def local(tokens, weight, old_left, old_right, selected, shaping, new_left, new_right):
@@ -412,12 +375,9 @@
     scalars = pl.BlockSpec(memory_space=pltpu.SMEM)
     upd, act = pl.pallas_call(
         kernel,
-        out_shape=(
-            jax.ShapeDtypeStruct((OWN, D), BF16),
-            jax.ShapeDtypeStruct((ROWS, COLS), BF16),
-        ),
+        out_shape=(pltpu.VMEM((OWN, D), BF16), pltpu.VMEM((ROWS, COLS), BF16)),
         in_specs=[anywhere] * 4 + [scalars] * 2 + [anywhere] * 2,
-        out_specs=(anywhere, anywhere),
+        out_specs=(pl.BlockSpec(memory_space=pltpu.VMEM),) * 2,
         scratch_shapes=[
             pltpu.VMEM((ROWS, D), BF16),
             pltpu.VMEM((2, 512, D), BF16),
@@ -437,9 +397,7 @@
             pltpu.VMEM((4, 8, 512), F32),
             pltpu.VMEM((4, 8, 512), F32),
             pltpu.VMEM((128, 512), BF16),
-            pltpu.VMEM((OWN, D), BF16),
-            pltpu.VMEM((ROWS, COLS), BF16),
-            dma((6,)), dma((9,)), dma((NCH,)), dma((3,)), dma((7,)), dma(()), dma(()), dma((6,)),
+            dma((6,)), dma((NCH,)), dma((3,)), dma((7,)), dma(()), dma(()), dma((6,)),
             dma((2, NCH)), dma((2, NCH)), dma((2, NCH)), dma((NCH,)), dma((NCH,)), dma((2, NCH)),
             dma((3,)), dma((4,)), dma((3,)), dma((8,)), dma((8,)), dma((8,)), dma((16,)), dma((2,)),
         ],

time: 85.8 us -> 63.4 us (0.74)
  Pallas kernels: 80.3 us -> 60.7 us
  local copies, waits for them, and re-layouts: 4.74 us -> 2.02 us
    pallas_call x1, Pallas kernels: 80.3 us -> 60.7 us  [local(): pl.pallas_call(kernel, out_shape=(pltpu.VMEM((OWN, D), BF16), pltpu.VMEM(...]
    unnamed x2, local copies, waits for them, and re-layouts: 4.74 us -> 2.02 us
where the time goes in v2:
time: 63.4 us
  Pallas kernels  60.7 us (96%)
  local copies, waits for them, and re-layouts  2.02 us (3%)
  between operations  0.64 us (1%)
    pallas_call x1, Pallas kernels, local(): pl.pallas_call(kernel, out_shape=(pltpu.VMEM((OWN, D), BF16), pltpu.VMEM(...  60.7 us
    unnamed x2, local copies, waits for them, and re-layouts  2.02 us

profile of v2, /device:TPU:1, one launch (start us, length us, event | category | flops | bytes accessed | tf_op | source)
XLA Modules:
  0.0 63.4 jit_solution(5599551848550895975)
XLA Ops:
  0.6 60.7 %gather_and_project.1 = (bf16[64,4096]{1,0:T(8,128)(2,1)S(1)}, bf16[896,1024]{1,0:T(8,128)(2,1)S(1)}) custom-call(bf16[896,4096]{1,0:T(8,128)(2,1)} %tok_h.1, bf16[64,4096]{1,0:T(8,128)(2,1)} %bitcast.3, bf16[112,4,256]{2,1,0:T(4,128)(2,1)} %oldl_h.1, bf16[112,4,1024]{2,1,0:T(4,128)(2,1)} %oldr_h.1, s32[1,8]{1,0:T(1,128)} %sel.1, f32[1,8]{1,0:T(1,128)} %shp.1, ...), custom_call_target="tpu_custom_call" | custom-call | tf_op jit(solution)/shard_map/gather_and_project/pallas_call | solution.py:376
  61.3 0.8 %copy.12 = bf16[4096,64]{0,1:T(8,128)(2,1)} copy(bf16[4096,64]{0,1:T(8,128)(2,1)S(1)} %bitcast.2) | data formatting | bytes 1048576
  62.1 1.2 %copy.13 = bf16[896,1024]{1,0:T(8,128)(2,1)} copy(bf16[896,1024]{1,0:T(8,128)(2,1)S(1)} %get-tuple-element.7) | data formatting | bytes 3670016

commit v3 on v2

--- a/solution.py
+++ b/solution.py
@@ -25,34 +25,39 @@
 NCH = CHUNKS + 1
 noise_scale = 0.5
 ORDER = (
-    ("start_left",), ("own_y", 0), ("own_y", 1), ("own_y", 2), ("own_y", 3), ("pick_right",), ("own_y", 8),
-    ("own_y", 4), ("own_y", 5), ("own_y", 6), ("own_y", 7), ("build_new",), ("proj_part",), ("own_z", 0),
-    ("own_z", 1), ("own_z", 2), ("own_z", 3), ("got_m", 0, 0), ("left_own",), ("proj_x",), ("got_p", 0, 0),
-    ("got_m", 0, 1), ("got_p", 0, 1), ("own_z", 8), ("own_z", 4), ("got_m", 0, 2), ("pass_z", 0), ("pass_z", 1),
-    ("got_p", 0, 2), ("got_m", 0, 3), ("got_p", 0, 3), ("got_m", 0, 8), ("pass_z", 2), ("pass_z", 3),
-    ("left_x", "m", 0), ("left_x", "p", 0), ("left_p", 1), ("left_m", 1), ("got_p", 0, 8), ("proj_z",),
-    ("got_p", 0, 4), ("got_m", 0, 4), ("got_m", 0, 5), ("got_p", 0, 5), ("got_m", 0, 6), ("pass_z", 4),
-    ("pass_z", 8), ("got_p", 0, 6), ("got_m", 0, 7), ("left_x", "2", 0), ("left_x", "m", 1), ("got_p", 0, 7),
-    ("got_2", 0, 1), ("left_x", "p", 1), ("other_y", 0), ("other_y", 1), ("left_x", "m", 5), ("got_2", 0, 0),
-    ("got_2", 0, 3), ("left_x", "p", 5), ("got_2", 0, 2), ("own_z", 5), ("own_z", 6), ("got_2", 0, 8),
-    ("other_y", 2), ("other_y", 3), ("got_2", 0, 4), ("left_p", 2), ("left_m", 2), ("got_2", 0, 5),
-    ("main_dot", 0, 0, 1), ("left_x", "2", 1), ("got_2", 0, 6), ("main_dot", 0, 2, 3), ("left_x", "2", 5),
-    ("got_2", 0, 7), ("own_z", 7), ("got_p", 1, 0), ("got_r", 0), ("got_m", 1, 0), ("other_y", 4), ("other_y", 8),
-    ("main_dot", 0, 4, 5), ("got_m", 1, 1), ("got_p", 1, 1), ("got_p", 1, 2), ("left_x", "m", 2), ("left_x", "p", 2),
-    ("got_m", 1, 2), ("main_dot", 0, 6, 7), ("left_m", 3), ("left_p", 3), ("left_x", "m", 6), ("left_x", "p", 6),
-    ("got_m", 1, 3), ("pass_z", 5), ("pass_z", 6), ("got_p", 1, 3), ("got_2", 1, 0), ("got_m", 1, 4),
-    ("got_p", 1, 4), ("got_m", 1, 8), ("pass_z", 7), ("left_x", "2", 2), ("got_p", 1, 8), ("got_2", 1, 1),
-    ("got_2", 1, 2), ("left_x", "m", 7), ("left_p", 4), ("left_x", "p", 7), ("got_2", 1, 3), ("left_x", "m", 3),
-    ("left_x", "p", 3), ("main_dot", 1, 0, 1), ("other_y", 5), ("left_x", "2", 6), ("got_2", 1, 8), ("got_2", 1, 4),
-    ("t_dot", 0), ("other_y", 6), ("main_dot", 1, 2, 3), ("other_y", 7), ("left_x", "2", 7), ("left_x", "p", 4),
-    ("left_x", "m", 4), ("got_r", 1), ("make_rt",), ("update", 0), ("left_x", "2", 3), ("got_m", 1, 5),
-    ("got_p", 1, 5), ("t_dot", 1), ("got_m", 1, 6), ("got_p", 1, 6), ("t_dot", 2), ("left_x", "2", 4),
-    ("got_m", 1, 7), ("got_p", 1, 7), ("update", 1), ("update", 2), ("got_2", 1, 5), ("t_dot", 3), ("got_2", 1, 6),
-    ("t_right", 0), ("t_right", 1), ("got_2", 1, 7), ("update", 3), ("main_dot", 1, 4, 5), ("finish", 0),
-    ("main_dot", 1, 6), ("main_dot", 1, 7), ("finish", 1),
+    ("start_left",), ("own_y", 0), ("own_z", 0), ("own_y", 1), ("own_z", 1), ("own_y", 2), ("own_y", 3),
+    ("pick_right",), ("own_y", 8), ("own_y", 4), ("build_new",), ("proj_part",), ("own_z", 2), ("own_z", 3),
+    ("own_y", 5), ("own_z", 8), ("own_z", 4), ("own_y", 6), ("own_z", 5), ("own_z", 6), ("own_y", 7), ("pass_z", 0),
+    ("left_own",), ("got_m", 0, 0), ("proj_x",), ("got_p", 0, 0), ("got_m", 0, 1), ("got_p", 0, 1), ("got_m", 0, 2),
+    ("got_p", 0, 2), ("pass_z", 1), ("got_m", 0, 3), ("got_p", 0, 3), ("left_x", "m", 0), ("left_x", "p", 0),
+    ("got_m", 0, 8), ("got_p", 0, 8), ("got_m", 0, 4), ("got_p", 0, 4), ("left_z", 6), ("pass_z", 2), ("left_z", 5),
+    ("got_m", 0, 5), ("got_p", 0, 5), ("pass_z", 3), ("other_y", 0), ("got_m", 0, 6), ("left_x", "2", 0),
+    ("got_p", 0, 6), ("got_m", 0, 7), ("got_p", 0, 7), ("left_z", 2), ("left_z", 1), ("left_x", "m", 6),
+    ("left_x", "p", 6), ("got_2", 0, 1), ("got_2", 0, 0), ("pass_z", 8), ("left_x", "m", 5), ("left_x", "p", 5),
+    ("got_2", 0, 3), ("left_z", 7), ("got_2", 0, 2), ("other_y", 1), ("got_2", 0, 8), ("proj_z",), ("got_2", 0, 4),
+    ("pass_z", 4), ("main_dot", 0, 0, 1), ("got_2", 0, 5), ("left_x", "m", 2), ("left_x", "p", 2), ("got_p", 1, 0),
+    ("main_dot", 0, 2, 3), ("left_z", 3), ("left_x", "m", 1), ("own_z", 7), ("left_x", "p", 1), ("got_m", 1, 0),
+    ("got_2", 0, 6), ("other_y", 2), ("got_r", 0), ("pass_z", 5), ("left_x", "2", 5), ("left_x", "2", 6),
+    ("got_2", 0, 7), ("got_p", 1, 1), ("other_y", 3), ("main_dot", 0, 4, 5), ("left_x", "m", 7), ("left_x", "p", 7),
+    ("got_m", 1, 1), ("pass_z", 6), ("left_z", 4), ("left_x", "2", 2), ("got_2", 1, 0), ("main_dot", 0, 6, 7),
+    ("left_x", "m", 3), ("got_m", 1, 2), ("left_x", "p", 3), ("got_p", 1, 2), ("pass_z", 7), ("other_y", 8),
+    ("t_dot", 0), ("left_x", "2", 1), ("got_m", 1, 3), ("got_p", 1, 3), ("left_x", "2", 7), ("got_2", 1, 1),
+    ("other_y", 4), ("left_x", "p", 4), ("left_x", "m", 4), ("got_2", 1, 2), ("left_x", "2", 3), ("got_m", 1, 8),
+    ("main_dot", 1, 0, 1), ("other_y", 5), ("got_p", 1, 8), ("t_dot", 1), ("other_y", 6), ("got_2", 1, 3),
+    ("t_dot", 2), ("left_x", "2", 4), ("got_m", 1, 4), ("got_p", 1, 4), ("other_y", 7), ("got_2", 1, 8),
+    ("main_dot", 1, 2, 3), ("got_p", 1, 5), ("t_dot", 3), ("got_m", 1, 5), ("got_p", 1, 6), ("got_m", 1, 6),
+    ("got_r", 1), ("make_rt",), ("t_right", 0), ("t_right", 1), ("got_2", 1, 4), ("update", 0), ("update", 1),
+    ("got_m", 1, 7), ("update", 2), ("update", 3), ("got_p", 1, 7), ("finish", 0), ("got_2", 1, 5), ("got_2", 1, 6),
+    ("main_dot", 1, 4, 5), ("got_2", 1, 7), ("main_dot", 1, 6), ("main_dot", 1, 7), ("finish", 1),
 )
 FACTOR = 1.0 / math.sqrt(D * RANK * SEL * 16)
 SIDE = noise_scale / math.sqrt(D * RANK)
+
+
+def batch(s, k):
+    if s == 0:
+        return k // 2
+    return 5 + (k // 2 if k < 6 else k - 3)
 
 
 def going_up(k):
@@ -73,7 +78,7 @@
     tok, wall, rall, lall, trw, trr, oldl, oldr, newl, newr, nl, nr,
     acc, tacc, tb, cx, cz, rt,
     ld, ssw, sly, slz, slx, sls, spx,
-    rp, rm, r2, tz, rz, dd, ly, lzp, lzm, lxp, lxm, lx2, dl, px,
+    rp, rm, r2, tz, rz, dd, ly, lz, lxp, lxm, lx2, dl, px,
 ):
     pop, col = lax.axis_index("pop"), lax.axis_index("col")
     y, zh, core = pop // 4, (pop // 2) % 2, pop % 2
@@ -91,7 +96,7 @@
     def zdev(step):
         return dev(y, (z + step + 8) % 8, core, x)
 
-    Zp1, Zm1, Zp2, Zm2 = zdev(1), zdev(-1), zdev(2), zdev(-2)
+    Zp1, Zm1, Zp2, Zm2, Zp3, Zm3 = [zdev(step) for step in (1, -1, 2, -2, 3, -3)]
     Sib = dev(y, z, 1 - core, x)
     Zl = [dev(y, zh * 4 + (zlo + j) % 4, core, x) for j in (1, 2, 3)]
 
@@ -136,7 +141,7 @@
         loads[i].start()
 
     barrier = pltpu.get_barrier_semaphore()
-    partners = [Yp, Ym, Yo, Xp, Xm, Xo, Zp1, Zm1, Zp2, Zm2, Sib] + Zl
+    partners = [Yp, Ym, Yo, Xp, Xm, Xo, Zp1, Zm1, Zp2, Zm2, Zp3, Zm3, Sib] + Zl
     for to in partners:
         pl.semaphore_signal(barrier, inc=1, device_id=to, device_id_type=MESH)
 
@@ -156,54 +161,53 @@
     def start_left():
         src = lall.at[col, pl.ds(lrow, 32), :]
         for j, to in enumerate((Yp, Ym, Yo)):
-            send(src, src, sly.at[j], ly.at[j], to)
+            send(src, src, sly, ly, to)
 
     def own_y(k):
         src = piece(zh, y, k)
-        send(src, src, ssw.at[k], rp.at[0, k], Yp)
-        send(src, src, ssw.at[k], rm.at[0, k], Ym)
-        send(src, src, ssw.at[k], dd.at[0, k], Sib)
+        send(src, src, ssw.at[k // 4], rp.at[0, k], Yp)
+        send(src, src, ssw.at[k // 4], rm.at[0, k], Ym)
+        send(src, src, ssw.at[k // 4], dd.at[batch(0, k)], Sib)
 
     def own_z(k):
-        send(piece(zh, y, k), transit(k), ssw.at[k], tz.at[k], Zp2 if going_up(k) else Zm2)
+        send(piece(zh, y, k), transit(k), ssw.at[k // 4], tz.at[k], Zp1 if going_up(k) else Zm1)
 
     def pass_z(k):
         arrived(transit(k), tz.at[k])
-        step = -2 if going_up(k) else 2
-        from_zh = ((z + step + 8) % 8) // 4
-        send(transit(k), piece(from_zh, y, k), ssw.at[k], rz.at[k], Zp2 if going_up(k) else Zm2)
+        from_zh = ((z + (7 if going_up(k) else 1)) % 8) // 4
+        send(transit(k), piece(from_zh, y, k), ssw.at[k // 4], rz.at[k], Zp3 if going_up(k) else Zm3)
 
     def other_y(k):
         src = piece(1 - zh, y, k)
         arrived(src, rz.at[k])
-        send(src, src, ssw.at[k], rp.at[1, k], Yp)
-        send(src, src, ssw.at[k], rm.at[1, k], Ym)
-        send(src, src, ssw.at[k], dd.at[1, k], Sib)
+        send(src, src, ssw.at[k // 4], rp.at[1, k], Yp)
+        send(src, src, ssw.at[k // 4], rm.at[1, k], Ym)
+        send(src, src, ssw.at[k // 4], dd.at[batch(1, k)], Sib)
 
     def got_p(s, k):
         h_ = zh if s == 0 else 1 - zh
         src = piece(h_, ym, k)
         arrived(src, rp.at[s, k])
         if going_up(k):
-            send(src, src, ssw.at[k], r2.at[s, k], Yp)
-        send(src, src, ssw.at[k], dd.at[s, k], Sib)
+            send(src, src, ssw.at[k // 4], r2.at[s, k], Yp)
+        send(src, src, ssw.at[k // 4], dd.at[batch(s, k)], Sib)
 
     def got_m(s, k):
         h_ = zh if s == 0 else 1 - zh
         src = piece(h_, yp, k)
         arrived(src, rm.at[s, k])
         if not going_up(k):
-            send(src, src, ssw.at[k], r2.at[s, k], Ym)
-        send(src, src, ssw.at[k], dd.at[s, k], Sib)
+            send(src, src, ssw.at[k // 4], r2.at[s, k], Ym)
+        send(src, src, ssw.at[k // 4], dd.at[batch(s, k)], Sib)
 
     def got_2(s, k):
         h_ = zh if s == 0 else 1 - zh
         src = piece(h_, yo, k)
         arrived(src, r2.at[s, k])
-        send(src, src, ssw.at[k], dd.at[s, k], Sib)
+        send(src, src, ssw.at[k // 4], dd.at[batch(s, k)], Sib)
 
     def got_r(s):
-        arrived(rall.at[0:128, :], dd.at[s, RCH])
+        arrived(rall.at[0:128, :], dd.at[batch(s, RCH)])
 
     def z_of(i):
         return z if i == 0 else ((z + 8 - i) % 8 if i <= 4 else (z + i - 4) % 8)
@@ -212,39 +216,34 @@
         src = lpiece(z_of(i), x)
         send(src, src, slx, lxp.at[i], Xp)
         send(src, src, slx, lxm.at[i], Xm)
-        send(src, src, sls, dl.at[(z_of(i) % 4) * 4 + x], Sib)
+        send(src, src, sls, dl.at[0], Sib)
 
     def left_own():
-        for j, y_ in enumerate((ym, yp, yo)):
-            arrived(lall.at[col, pl.ds(pl.multiple_of((zh * 2 + core) * 128 + y_ * 32, 32), 32), :], ly.at[j])
+        arrived(lall.at[0, 0:96, :], ly)
         src = lpiece(z, x)
-        send(src, src, slz.at[0], lzp.at[0], Zp1)
-        send(src, src, slz.at[1], lzm.at[0], Zm1)
+        for i, to in ((2, Zp2), (6, Zm2), (1, Zp1), (5, Zm1)):
+            send(src, src, slz, lz.at[i - 1], to)
         left_out(0)
 
-    def left_p(d):
-        src = lpiece(z_of(d), x)
-        arrived(src, lzp.at[d - 1])
-        if d < 4:
-            send(src, src, slz.at[1 + d], lzp.at[d], Zp1)
-        left_out(d)
-
-    def left_m(d):
-        src = lpiece(z_of(4 + d), x)
-        arrived(src, lzm.at[d - 1])
-        if d < 3:
-            send(src, src, slz.at[4 + d], lzm.at[d], Zm1)
-        left_out(4 + d)
+    def left_z(i):
+        src = lpiece(z_of(i), x)
+        arrived(src, lz.at[i - 1])
+        if i == 2:
+            send(src, src, slz, lz.at[2], Zp1)
+            send(src, src, slz, lz.at[3], Zp2)
+        if i == 6:
+            send(src, src, slz, lz.at[6], Zm1)
+        left_out(i)
 
     def left_x(which, i):
-        x_, sem = {"p": (xm, lxp), "m": (xp, lxm), "2": (xo, lx2)}[which]
+        x_, sem, j = {"p": (xm, lxp, 1), "m": (xp, lxm, 2), "2": (xo, lx2, 3)}[which]
         src = lpiece(z_of(i), x_)
         arrived(src, sem.at[i])
         if which == "p" and i % 2 == 0:
             send(src, src, slx, lx2.at[i], Xp)
         if which == "m" and i % 2 == 1:
             send(src, src, slx, lx2.at[i], Xm)
-        send(src, src, sls, dl.at[(z_of(i) % 4) * 4 + x_], Sib)
+        send(src, src, sls, dl.at[j], Sib)
 
     def pick_right():
         loads[2].wait()
@@ -285,15 +284,15 @@
             part = jnp.where(own_member(n), part, 0.0)
             cx[x, :, 128 * g:128 * (g + 1)] = part.reshape(n // 8, 8, 128).sum(axis=0)
         src = cx.at[x]
-        for j, to in enumerate((Xp, Xm, Xo)):
-            send(src, src, spx.at[j], px.at[0], to)
+        for to in (Xp, Xm, Xo):
+            send(src, src, spx.at[0], px.at[0], to)
 
     def proj_x():
         arrived(cx.at[0:3], px.at[0])
         cz[zlo] = (cx[0] + cx[1]) + (cx[2] + cx[3])
         src = cz.at[zlo]
-        for j, to in enumerate(Zl):
-            send(src, src, spx.at[3 + j], px.at[1], to)
+        for to in Zl:
+            send(src, src, spx.at[1], px.at[1], to)
 
     def proj_z():
         arrived(cz.at[0:3], px.at[1])
@@ -307,9 +306,8 @@
 
     def main_dot(s, *ks):
         h_ = zh if s == 0 else 1 - zh
-        for k in ks:
-            arrived(wall.at[h_, 0:256, k * LEN:(k + 1) * LEN], dd.at[s, k])
         deep = slice(ks[0] * LEN, (ks[-1] + 1) * LEN)
+        arrived(wall.at[h_, 0:256, deep], dd.at[batch(s, ks[0])])
         for n in range(2):
             at = slice(n * 256, (n + 1) * 256)
             acc[h_, :, at] += nt(tok[:, deep], wall[h_, at, deep])
@@ -321,8 +319,7 @@
 
     def t_dot(j):
         cs = [zlo_ * 4 + xs[j] for zlo_ in range(4)]
-        for c in cs:
-            arrived(lall.at[c, 0:256, :], dl.at[c])
+        arrived(lall.at[0:2], dl.at[j])
         part = sum(nt(tok[:, slab(c)], lall[c]) for c in cs)
         tacc[...] = part if j == 0 else tacc[...] + part
 
@@ -351,22 +348,29 @@
             outv[:, at] = (pre * pre).astype(BF16)
 
     steps = {f.__name__: f for f in (
-        start_left, own_y, own_z, pass_z, other_y, got_p, got_m, got_2, got_r, left_own, left_p, left_m, left_x,
+        start_left, own_y, own_z, pass_z, other_y, got_p, got_m, got_2, got_r, left_own, left_z, left_x,
         pick_right, build_new, proj_part, proj_x, proj_z, main_dot, t_dot, make_rt, update, t_right, finish,
     )}
     for name, *rest in ORDER:
         steps[name](*rest)
 
-    for k in range(NCH):
-        sent(wall.at[:, :, 0:LEN], ssw.at[k])
-    for j in range(3):
-        sent(lall.at[0, 0:32, :], sly.at[j])
-    for j in range(7):
-        sent(lall.at[0, 0:128, :], slz.at[j])
+    for half in range(2):
+        sent(wall.at[half], ssw.at[half])
+    sent(wall.at[:, :, 0:LEN], ssw.at[2])
+    sent(lall.at[0, 0:96, :], sly)
+    sent(wall.at[0, 0:448, 0:LEN], slz)
     sent(lall.at[0:6], slx)
     sent(lall.at[0:8], sls)
-    for j in range(6):
-        sent(cx.at[0], spx.at[j])
+    for j in range(2):
+        sent(cx.at[0:3], spx.at[j])
+
+
+def write_out(upd, act, upd_h, act_h, sem):
+    copies = [pltpu.make_async_copy(act, act_h, sem.at[0]), pltpu.make_async_copy(upd, upd_h, sem.at[1])]
+    for copy in copies:
+        copy.start()
+    for copy in copies:
+        copy.wait()
 
 
 def local(tokens, weight, old_left, old_right, selected, shaping, new_left, new_right):
@@ -397,15 +401,27 @@
             pltpu.VMEM((4, 8, 512), F32),
             pltpu.VMEM((4, 8, 512), F32),
             pltpu.VMEM((128, 512), BF16),
-            dma((6,)), dma((NCH,)), dma((3,)), dma((7,)), dma(()), dma(()), dma((6,)),
-            dma((2, NCH)), dma((2, NCH)), dma((2, NCH)), dma((NCH,)), dma((NCH,)), dma((2, NCH)),
-            dma((3,)), dma((4,)), dma((3,)), dma((8,)), dma((8,)), dma((8,)), dma((16,)), dma((2,)),
+            dma((6,)), dma((3,)), dma(()), dma(()), dma(()), dma(()), dma((2,)),
+            dma((2, NCH)), dma((2, NCH)), dma((2, NCH)), dma((NCH,)), dma((NCH,)), dma((11,)),
+            dma(()), dma((7,)), dma((8,)), dma((8,)), dma((8,)), dma((4,)), dma((2,)),
         ],
         compiler_params=pltpu.CompilerParams(
             collective_id=0, has_side_effects=True, vmem_limit_bytes=56 * 1024 * 1024
         ),
         name="gather_and_project",
     )(tokens, weight.T, old_left, old_right, selected, shaping, new_left, new_right)
+    upd, act = pl.pallas_call(
+        write_out,
+        out_shape=(
+            jax.ShapeDtypeStruct((OWN, D), BF16),
+            jax.ShapeDtypeStruct((ROWS, COLS), BF16),
+        ),
+        in_specs=[pl.BlockSpec(memory_space=pltpu.VMEM)] * 2,
+        out_specs=(anywhere, anywhere),
+        scratch_shapes=[dma((2,))],
+        compiler_params=pltpu.CompilerParams(vmem_limit_bytes=8 * 1024 * 1024),
+        name="write_out",
+    )(upd, act)
     return (upd.T, act)
 
 

time: 63.4 us -> 61.2 us (0.965)
  local copies, waits for them, and re-layouts: 2.02 us -> 0 us
    unnamed x2 -> x0, local copies, waits for them, and re-layouts: 2.02 us -> none
    pallas_call x1, Pallas kernels: 60.7 us -> 59.1 us  [local(): pl.pallas_call(kernel, out_shape=(pltpu.VMEM((OWN, D), BF16), pltpu.VMEM(...]
    pallas_call x0 -> x1, Pallas kernels: none -> 1.42 us  [local(): pl.pallas_call(write_out, out_shape=(jax.ShapeDtypeStruct((OWN, D), BF16)...]
where the time goes in v3:
time: 61.2 us; the launch traced here: 61.1 us
  Pallas kernels  60.5 us (99%)
  between operations  0.64 us (1%)
    pallas_call x1, Pallas kernels, local(): pl.pallas_call(kernel, out_shape=(pltpu.VMEM((OWN, D), BF16), pltpu.VMEM(...  59.1 us
    pallas_call x1, Pallas kernels, local(): pl.pallas_call(write_out, out_shape=(jax.ShapeDtypeStruct((OWN, D), BF16)...  1.42 us

profile of v3, /device:TPU:1, one launch (start us, length us, event | category | flops | bytes accessed | tf_op | source)
XLA Modules:
  0.0 61.1 jit_solution(15105490811649170864)
XLA Ops:
  0.6 59.1 %gather_and_project.1 = (bf16[64,4096]{1,0:T(8,128)(2,1)S(1)}, bf16[896,1024]{1,0:T(8,128)(2,1)S(1)}) custom-call(bf16[896,4096]{1,0:T(8,128)(2,1)} %tok_h.1, bf16[64,4096]{1,0:T(8,128)(2,1)} %bitcast.2, bf16[112,4,256]{2,1,0:T(4,128)(2,1)} %oldl_h.1, bf16[112,4,1024]{2,1,0:T(4,128)(2,1)} %oldr_h.1, s32[1,8]{1,0:T(1,128)} %sel.1, f32[1,8]{1,0:T(1,128)} %shp.1, ...), custom_call_target="tpu_custom_call" | custom-call | tf_op jit(solution)/shard_map/gather_and_project/pallas_call | solution.py:380
  59.7 1.4 %write_out.1 = (bf16[64,4096]{1,0:T(8,128)(2,1)}, bf16[896,1024]{1,0:T(8,128)(2,1)}) custom-call(bf16[64,4096]{1,0:T(8,128)(2,1)S(1)} %get-tuple-element.6.upd, bf16[896,1024]{1,0:T(8,128)(2,1)S(1)} %get-tuple-element.7.act), custom_call_target="tpu_custom_call" | custom-call | tf_op jit(solution)/shard_map/write_out/pallas_call | solution.py:413

commit v4 on v3

--- a/solution.py
+++ b/solution.py
@@ -48,7 +48,7 @@
     ("main_dot", 1, 2, 3), ("got_p", 1, 5), ("t_dot", 3), ("got_m", 1, 5), ("got_p", 1, 6), ("got_m", 1, 6),
     ("got_r", 1), ("make_rt",), ("t_right", 0), ("t_right", 1), ("got_2", 1, 4), ("update", 0), ("update", 1),
     ("got_m", 1, 7), ("update", 2), ("update", 3), ("got_p", 1, 7), ("finish", 0), ("got_2", 1, 5), ("got_2", 1, 6),
-    ("main_dot", 1, 4, 5), ("got_2", 1, 7), ("main_dot", 1, 6), ("main_dot", 1, 7), ("finish", 1),
+    ("main_dot", 1, 4, 5), ("got_2", 1, 7), ("main_dot", 1, 6), ("last_dot", 7),
 )
 FACTOR = 1.0 / math.sqrt(D * RANK * SEL * 16)
 SIDE = noise_scale / math.sqrt(D * RANK)
@@ -340,16 +340,28 @@
             at = slice(n * 256, (n + 1) * 256)
             acc[h_, :, at] += nn(tb[...], rall[:, h_ * 512 + n * 256:h_ * 512 + (n + 1) * 256])
 
+    def put(h_, y_, pre):
+        at = pl.ds(pl.multiple_of((2 * y_ + h_) * 128, 128), 128)
+        pre = jnp.maximum(pre, 0.0)
+        outv[:, at] = (pre * pre).astype(BF16)
+
     def finish(s):
         h_ = zh if s == 0 else 1 - zh
         for y_ in range(4):
-            at = pl.ds(pl.multiple_of((2 * y_ + h_) * 128, 128), 128)
-            pre = jnp.maximum(acc[h_, :, y_ * 128:(y_ + 1) * 128], 0.0)
-            outv[:, at] = (pre * pre).astype(BF16)
+            put(h_, y_, acc[h_, :, y_ * 128:(y_ + 1) * 128])
+
+    def last_dot(k):
+        h_, deep = 1 - zh, slice(k * LEN, (k + 1) * LEN)
+        arrived(wall.at[h_, 0:256, deep], dd.at[batch(1, k)])
+        for n in range(2):
+            at = slice(n * 256, (n + 1) * 256)
+            pre = acc[h_, :, at] + nt(tok[:, deep], wall[h_, at, deep])
+            for j in range(2):
+                put(h_, 2 * n + j, pre[:, j * 128:(j + 1) * 128])
 
     steps = {f.__name__: f for f in (
         start_left, own_y, own_z, pass_z, other_y, got_p, got_m, got_2, got_r, left_own, left_z, left_x,
-        pick_right, build_new, proj_part, proj_x, proj_z, main_dot, t_dot, make_rt, update, t_right, finish,
+        pick_right, build_new, proj_part, proj_x, proj_z, main_dot, t_dot, make_rt, update, t_right, finish, last_dot,
     )}
     for name, *rest in ORDER:
         steps[name](*rest)

time: 61.2 us -> 61.3 us (level)
  no operation moved by 1% of the time
where the time goes in v4:
time: 61.3 us
  Pallas kernels  60.6 us (99%)
  between operations  0.64 us (1%)
    pallas_call x1, Pallas kernels, local(): pl.pallas_call(kernel, out_shape=(pltpu.VMEM((OWN, D), BF16), pltpu.VMEM(...  59.2 us
    pallas_call x1, Pallas kernels, local(): pl.pallas_call(write_out, out_shape=(jax.ShapeDtypeStruct((OWN, D), BF16)...  1.42 us

profile of v4, /device:TPU:1, one launch (start us, length us, event | category | flops | bytes accessed | tf_op | source)
XLA Modules:
  0.0 61.3 jit_solution(8505894895452515458)
XLA Ops:
  0.6 59.2 %gather_and_project.1 = (bf16[64,4096]{1,0:T(8,128)(2,1)S(1)}, bf16[896,1024]{1,0:T(8,128)(2,1)S(1)}) custom-call(bf16[896,4096]{1,0:T(8,128)(2,1)} %tok_h.1, bf16[64,4096]{1,0:T(8,128)(2,1)} %bitcast.2, bf16[112,4,256]{2,1,0:T(4,128)(2,1)} %oldl_h.1, bf16[112,4,1024]{2,1,0:T(4,128)(2,1)} %oldr_h.1, s32[1,8]{1,0:T(1,128)} %sel.1, f32[1,8]{1,0:T(1,128)} %shp.1, ...), custom_call_target="tpu_custom_call" | custom-call | tf_op jit(solution)/shard_map/gather_and_project/pallas_call | solution.py:392
  59.8 1.4 %write_out.1 = (bf16[64,4096]{1,0:T(8,128)(2,1)}, bf16[896,1024]{1,0:T(8,128)(2,1)}) custom-call(bf16[64,4096]{1,0:T(8,128)(2,1)S(1)} %get-tuple-element.6.upd, bf16[896,1024]{1,0:T(8,128)(2,1)S(1)} %get-tuple-element.7.act), custom_call_target="tpu_custom_call" | custom-call | tf_op jit(solution)/shard_map/write_out/pallas_call | solution.py:425
